TPU v7x, 512 devices: a whole 4x4x16 slice. The times are simulated.
512 devices in a mesh: tm: 32 (over z, y_hi), lat: 16 (over x, y_lo, core).
Axes of the slice: x: 4, y: 4 (y_hi: 2, y_lo: 2; y = y_hi * 2 + y_lo), z: 16, core: 2. Of those that a mesh axis runs over, the one named last changes fastest.
Arguments:
- controls: float32 [32, 3, 512, 1024], P('tm', None, 'lat'), may hold values from -3 to 3
- background: float32 [3, 512, 1024], P(None, 'lat'), may hold values from -3 to 3
- observations: float32 [32, 4, 512, 1024], P('tm', None, 'lat'), may hold values from -3 to 3
- obs_count: int32 [32, 4, 512, 1024], P('tm', None, 'lat'), may hold values from 0 to 3
Outputs:
- slid_controls: float32 [32, 3, 512, 1024], P('tm', None, 'lat')
- gradient: float32 [32, 3, 512, 1024], P('tm', None, 'lat')
- cost: float32 [], replicated
All inputs are finite; a program needn't handle non-finite values.
Results may differ from a plain program's by a relative error of at most 0.0001.
Values sent between devices are 32-bit elements; how exact they have to be, the bound alone decides.
A program may use at most 64 MiB of HBM per device.

v0:
```python
import jax
import jax.numpy as jnp
from jax import lax
from jax.sharding import Mesh
from jax.sharding import PartitionSpec as P

LAT = ("lat_0", "lat_1", "lat_2")
TM = ("tm_0", "tm_1")
TM_LAT = ("tm_0", "tm_1", "lat_0", "lat_1", "lat_2")
courant = 0.25
diffusion = 0.1
spin_scale = 0.3
obs_weight = 0.5
q_weight = 1.0
step_scale = 0.2
epsilon = 1e-06


def extended_2(cells, sides, width):
    for axis, dim in sides:
        count = lax.axis_size(axis)
        ends = count - 1
        head = lax.slice_in_dim(cells, 0, width, axis=dim)
        tail = lax.slice_in_dim(cells, cells.shape[dim] - width, cells.shape[dim], axis=dim)
        cells = jnp.concatenate(
            [
                lax.ppermute(tail, axis, [(i, (i + 1) % count) for i in range(ends)]),
                cells,
                lax.ppermute(head, axis, [((i + 1) % count, i) for i in range(ends)]),
            ],
            axis=dim,
        )
    return cells


def from_behind(block, axis, distance):
    devices = range(lax.axis_size(axis))
    route = [(i - distance, i) for i in devices if i - distance in devices]
    return lax.ppermute(block, axis, route)


def by_axis(x, axes):
    for axis in axes:
        x = lax.psum(x, axis)
    return x


def advance(extended, coriolis):
    center = extended[:, 1:-1]
    north = extended[:, 2:]
    south = extended[:, :-2]
    east = jnp.roll(center, -1, axis=2)
    west = jnp.roll(center, 1, axis=2)
    height, zonal, merid = (center[0], center[1], center[2])
    flux_east = east[1] * (1.0 + east[0])
    flux_west = west[1] * (1.0 + west[0])
    flux_north = north[2] * (1.0 + north[0])
    flux_south = south[2] * (1.0 + south[0])
    spread = north + south + east + west - 4.0 * center
    half = 0.5 * courant
    new_height = (
        height - half * (flux_east - flux_west + flux_north - flux_south) + diffusion * spread[0]
    )
    new_zonal = (
        zonal
        - half * (east[0] - west[0])
        + coriolis * merid
        - half * (zonal * (east[1] - west[1]) + merid * (north[1] - south[1]))
        + diffusion * spread[1]
    )
    new_merid = (
        merid
        - half * (north[0] - south[0])
        - coriolis * zonal
        - half * (zonal * (east[2] - west[2]) + merid * (north[2] - south[2]))
        + diffusion * spread[2]
    )
    return jnp.stack([new_height, new_zonal, new_merid])


def coriolis_rows(index, total):
    latitude = jnp.pi * ((index.astype(jnp.float32) + 0.5) / total - 0.5)
    return (spin_scale * jnp.sin(latitude))[:, None]


def section_rows(current, first, margin, total):
    count = current.shape[1] - 2
    index = first - margin + jnp.arange(count, dtype=jnp.int32)
    valid = ((index >= 0) & (index < total)).astype(jnp.float32)[:, None]
    return advance(current, coriolis_rows(index, total)) * valid


def add_rims(wide, got, width):
    inner = wide[:, width:-width]
    count = inner.shape[1]
    lower = jnp.pad(got[:, :width], ((0, 0), (0, count - width), (0, 0)))
    upper = jnp.pad(got[:, -width:], ((0, 0), (count - width, 0), (0, 0)))
    return inner + lower + upper


def with_height(grad, inject):
    return grad + jnp.concatenate([inject[None], jnp.zeros_like(grad[1:])], axis=0)


def forward_deep(state, weights, targets, first, total):
    rows = state.shape[1]
    steps = targets.shape[0]
    current = extended_2(state, ((LAT, 1),), steps)
    inputs = []
    resids = []
    cost = jnp.zeros((), jnp.float32)
    for section in range(steps):
        margin = steps - 1 - section
        inputs.append(current)
        current = section_rows(current, first, margin, total)
        resid = current[0, margin : margin + rows] - targets[section]
        resids.append(weights[section] * resid)
        cost = cost + 0.5 * jnp.sum(weights[section] * resid * resid)
    return (current, cost, inputs, resids)


def backward_deep(start_grad, inputs, resids, first, total):
    steps = len(inputs)
    grad = start_grad
    for section in reversed(range(steps)):
        margin = steps - 1 - section
        grad = with_height(grad, jnp.pad(resids[section], ((margin, margin), (0, 0))))
        outputs, pull = jax.vjp(
            lambda current: section_rows(current, first, margin, total), inputs[section]
        )
        grad = pull(grad)[0]
    rims = jnp.concatenate([grad[:, :steps], grad[:, -steps:]], axis=1)
    got = extended_2(rims, ((LAT, 1),), steps)
    return add_rims(grad, got, steps)


def per_device(controls, background, observations, obs_count):
    state = controls[0]
    rows = state.shape[1]
    total = rows * lax.axis_size(LAT)
    first = lax.axis_index(LAT) * rows
    position = lax.axis_index(TM)
    windows = lax.axis_size(TM)
    weights = obs_weight * obs_count[0].astype(jnp.float32)
    targets = observations[0]
    following = from_behind(state, TM, -1)
    final, obs_cost, inputs, resids = forward_deep(state, weights, targets, first, total)
    received = from_behind(final, TM, 1)
    previous = jnp.where(position == 0, background, received)
    misfit = state - previous
    weighted = q_weight * misfit
    local_cost = obs_cost + 0.5 * q_weight * jnp.sum(misfit * misfit)
    later = jnp.where(
        position == windows - 1, jnp.zeros_like(final), q_weight * (following - final)
    )
    cost_total = by_axis(local_cost, TM_LAT)
    adjoint = backward_deep(-later, inputs, resids, first, total)
    gradient = weighted + adjoint
    squares = jnp.sum(gradient * gradient)
    square_total = by_axis(squares, TM_LAT)
    entries = float(windows * lax.axis_size(LAT) * state.size)
    norm = jnp.sqrt(square_total / entries + epsilon)
    updated = state - step_scale * gradient / norm
    arriving = from_behind(updated, TM, -1)
    slid = jnp.where(position == windows - 1, final, arriving)
    return (slid[None], gradient[None], cost_total)


def solution(mesh):
    finer = Mesh(mesh.devices.reshape(16, 2, 4, 2, 2), ("tm_0", "tm_1", "lat_0", "lat_1", "lat_2"))
    return jax.shard_map(
        per_device,
        mesh=finer,
        in_specs=(
            P(TM, None, LAT, None),
            P(None, LAT, None),
            P(TM, None, LAT, None),
            P(TM, None, LAT, None),
        ),
        out_specs=(P(TM, None, LAT, None), P(TM, None, LAT, None), P()),
        check_vma=False,
    )
```

profile of v0, /device:TPU:16, one launch (start us, length us, event | category | flops | bytes accessed | tf_op | source)
XLA Modules:
  0.0 145.0 jit_solution(15232609845705432557)
XLA Ops:
  0.6 7.6 %collective-permute-start.3 = (f32[3,32,1024]{2,1,0:T(8,128)}, f32[3,32,1024]{2,1,0:T(8,128)}, u32[]{:S(2)}, u32[]{:S(2)}) collective-permute-start(f32[3,32,1024]{2,1,0:T(8,128)} %bitcast.92), channel_id=1, source_target_pairs={{16,0},{32,16},{48,32},{64,48},{80,64},{96,80},{112,96},{128,112},... | collective-permute-start | bytes 1179656 | tf_op jit(solution)/shard_map/ppermute | solution.py:39
  8.2 1.0 fusion.121
  9.2 1.3 collective-permute-start
  10.5 1.3 collective-permute-start.1
  12.0 0.6 sine_multiply_fusion
  12.6 1.9 %convert_multiply_fusion = f32[1,4,32,1024]{3,2,1,0:T(8,128)} fusion(s32[1,4,32,1024]{3,2,1,0:T(8,128)} %param.7), kind=kLoop, calls=%fused_computation.32 | loop fusion | flops 262144 | bytes 1048576 | tf_op jit(solution)/shard_map/mul | solution.py:144
  14.6 0.5 and_convert_fusion
  16.0 0.8 fusion.41
  17.9 0.8 fusion.38
  20.0 0.8 fusion.35
  21.8 0.5 copy-done.56
  22.4 0.8 fusion.63
  23.4 0.4 copy-done.23
  23.8 0.8 maximum_multiply_fusion.3
  24.7 1.9 %collective-permute-start.2 = (f32[3,32,1024]{2,1,0:T(8,128)}, f32[3,32,1024]{2,1,0:T(8,128)}, u32[]{:S(2)}, u32[]{:S(2)}) collective-permute-start(f32[3,32,1024]{2,1,0:T(8,128)} %maximum_multiply_fusion.3), channel_id=1, source_target_pairs={{0,16},{16,32},{32,48},{48,64},{64,80},{80,96},{96,112},{112,128},... | collective-permute-start | bytes 1179656 | tf_op jit(solution)/shard_map/ppermute | solution.py:39
  26.6 2.4 %fusion.50 = (f32[]{:T(128)}, f32[]{:T(128)}, f32[]{:T(128)}, f32[]{:T(128)}, f32[32,1024]{1,0:T(8,128)S(1)}, /*index=5*/f32[32,1024]{1,0:T(8,128)S(1)}, f32[32,1024]{1,0:T(8,128)}) fusion(f32[3,32,1024]{2,1,0:T(8,128)} %maximum_multiply_fusion.3, f32[1,4,32,1024]{3,2,1,0:T(8,128)S(1)} %copy-done.12, f32[1,4,32,1024]{3,2,1,0:T(8,128)S(1)} %copy-done.43, ...), kind=kLoop, calls=%fused_computation.234 | loop fusion | flops 524284 | bytes 1966096 | tf_op jit(solution)/shard_map/reduce_sum | solution.py:118
  29.0 0.7 pad_bitcast_fusion.2
  29.7 0.7 pad_bitcast_fusion.1
  32.9 0.9 pad_bitcast_fusion
  33.9 1.1 fusion.66
  35.1 1.2 add_multiply_fusion.3
  36.7 0.7 copy-done.9
  38.0 0.7 copy-done.51
  39.1 0.8 copy-done.48
  40.1 0.8 copy-done.5
  41.1 0.3 fusion.76
  41.4 0.7 copy-done.3
  43.4 0.7 copy-done.47
  44.3 0.8 copy-done.1
  45.3 0.3 fusion.77
  45.6 0.5 copy-done.16
  47.4 0.6 copy-done.62
  48.2 0.6 copy-done.14
  49.0 0.3 fusion.78
  49.3 0.6 copy-done.36
  51.2 4.9 %collective-permute-start.4 = (f32[3,4,1024]{2,1,0:T(4,128)S(1)}, f32[3,4,1024]{2,1,0:T(4,128)S(1)}, u32[]{:S(2)}, u32[]{:S(2)}) collective-permute-start(f32[3,4,1024]{2,1,0:T(4,128)S(1)} %get-tuple-element.72), channel_id=1, source_target_pairs={{0,1},{1,2},{2,3},{3,4},{4,5},{5,6},{6,7},{7,8},{8,9},{9,10},{10,1... | collective-permute-start | bytes 147464 | tf_op jit(solution)/shard_map/ppermute | solution.py:27
  56.1 1.4 collective-permute-start.5
  57.7 1.7 %multiply_reduce_fusion = (f32[]{:T(128)}, f32[3,32,1024]{2,1,0:T(8,128)S(1)}) fusion(f32[3,32,1024]{2,1,0:T(8,128)S(1)} %copy-done.50, f32[3,32,1024]{2,1,0:T(8,128)} %collective-permute-done.2, pred[]{:T(512)S(6)} %eq.8, f32[1,3,32,1024]{3,2,1,0:T(8,128)S(1)} %copy-done.11), kind=kLoop, calls=%fused_computation.101 | loop fusion | flops 393215 | bytes 1572869 | tf_op jit(solution)/shard_map/reduce_sum | solution.py:152
  60.1 1.8 %collective-permute-done.5 = f32[3,4,1024]{2,1,0:T(4,128)S(1)} collective-permute-done((f32[3,4,1024]{2,1,0:T(4,128)S(1)}, f32[3,4,1024]{2,1,0:T(4,128)S(1)}, u32[]{:S(2)}, u32[]{:S(2)}) %collective-permute-start.5) | collective-permute-done | bytes 49184 | tf_op jit(solution)/shard_map/ppermute | solution.py:29
  61.9 0.7 multiply_reduce_fusion.1
  62.6 35.0 %all-reduce.137 = (f32[]{:T(128)}, f32[]{:T(128)}) all-reduce(f32[]{:T(128)} %get-tuple-element.22, f32[]{:T(128)S(6)} %add.788), channel_id=1, replica_groups=mesh['tm_0'=16,'tm_1'=2,'lat_0'=4,'lat_1'=2,'lat_2'=2] {'tm_0'}, use_global_device_ids=true, to_apply=%region_1.2 | all-reduce | flops 2 | bytes 16 | tf_op jit(solution)/shard_map/psum | solution.py:44
  97.6 7.1 %all-reduce.141 = (f32[]{:T(128)}, f32[]{:T(128)}) all-reduce(f32[]{:T(128)} %get-tuple-element.7, f32[]{:T(128)} %get-tuple-element.8), channel_id=1, replica_groups=mesh['tm_0'=16,'tm_1'=2,'lat_0'=4,'lat_1'=2,'lat_2'=2] {'tm_1'}, use_global_device_ids=true, to_apply=%region_2.3 | all-reduce | flops 2 | bytes 16 | tf_op jit(solution)/shard_map/psum | solution.py:44
  104.7 14.3 %all-reduce.138 = (f32[]{:T(128)}, f32[]{:T(128)}) all-reduce(f32[]{:T(128)} %get-tuple-element.15, f32[]{:T(128)} %get-tuple-element.16), channel_id=1, replica_groups=mesh['tm_0'=16,'tm_1'=2,'lat_0'=4,'lat_1'=2,'lat_2'=2] {'lat_0'}, use_global_device_ids=true, to_apply=%region_3.4 | all-reduce | flops 2 | bytes 16 | tf_op jit(solution)/shard_map/psum | solution.py:44
  119.0 5.6 %all-reduce.140 = (f32[]{:T(128)}, f32[]{:T(128)}) all-reduce(f32[]{:T(128)} %get-tuple-element.9, f32[]{:T(128)} %get-tuple-element.10), channel_id=1, replica_groups=mesh['tm_0'=16,'tm_1'=2,'lat_0'=4,'lat_1'=2,'lat_2'=2] {'lat_1'}, use_global_device_ids=true, to_apply=%region_4.5 | all-reduce | flops 2 | bytes 16 | tf_op jit(solution)/shard_map/psum | solution.py:44
  124.6 3.1 %all-reduce.139 = (f32[]{:T(128)}, f32[]{:T(128)}) all-reduce(f32[]{:T(128)} %get-tuple-element.13, f32[]{:T(128)} %get-tuple-element.14), channel_id=1, replica_groups=mesh['tm_0'=16,'tm_1'=2,'lat_0'=4,'lat_1'=2,'lat_2'=2] {'lat_2'}, use_global_device_ids=true, to_apply=%region_5.6 | all-reduce | flops 2 | bytes 16 | tf_op jit(solution)/shard_map/psum | solution.py:44
  128.5 2.2 %collective-permute-start.6 = (f32[3,32,1024]{2,1,0:T(8,128)S(1)}, f32[3,32,1024]{2,1,0:T(8,128)S(1)}, u32[]{:S(2)}, u32[]{:S(2)}) collective-permute-start(f32[3,32,1024]{2,1,0:T(8,128)S(1)} %divide_subtract_fusion), channel_id=1, source_target_pairs={{16,0},{32,16},{48,32},{64,48},{80,64},{96,80},{112,96},{128,112},... | collective-permute-start | bytes 1179656 | tf_op jit(solution)/shard_map/ppermute | solution.py:39
  130.7 13.4 %collective-permute-done.6 = f32[3,32,1024]{2,1,0:T(8,128)S(1)} collective-permute-done((f32[3,32,1024]{2,1,0:T(8,128)S(1)}, f32[3,32,1024]{2,1,0:T(8,128)S(1)}, u32[]{:S(2)}, u32[]{:S(2)}) %collective-permute-start.6) | collective-permute-done | bytes 393248 | tf_op jit(solution)/shard_map/ppermute | solution.py:39
  144.1 0.9 select_bitcast_fusion
  (195 shorter events, 10.7 us)
Async XLA Ops:
  0.6 34.4 %collective-permute-start.3 = (f32[3,32,1024]{2,1,0:T(8,128)}, f32[3,32,1024]{2,1,0:T(8,128)}, u32[]{:S(2)}, u32[]{:S(2)}) collective-permute-start(f32[3,32,1024]{2,1,0:T(8,128)} %bitcast.92), channel_id=1, source_target_pairs={{16,0},{32,16},{48,32},{64,48},{80,64},{96,80},{112,96},{128,112},... | collective-permute-start | bytes 1179656 | tf_op jit(solution)/shard_map/ppermute | solution.py:39
  9.2 5.9 %collective-permute-start = (f32[3,4,1024]{2,1,0:T(4,128)S(1)}, f32[3,4,1024]{2,1,0:T(4,128)S(1)}, u32[]{:S(2)}, u32[]{:S(2)}) collective-permute-start(f32[3,4,1024]{2,1,0:T(4,128)S(1)} %get-tuple-element.254), channel_id=1, source_target_pairs={{0,1},{1,2},{2,3},{3,4},{4,5},{5,6},{6,7},{7,8},{8,9},{9,10},{10,1... | collective-permute-start | bytes 147464 | tf_op jit(solution)/shard_map/ppermute | solution.py:27
  10.5 4.6 %collective-permute-start.1 = (f32[3,4,1024]{2,1,0:T(4,128)S(1)}, f32[3,4,1024]{2,1,0:T(4,128)S(1)}, u32[]{:S(2)}, u32[]{:S(2)}) collective-permute-start(f32[3,4,1024]{2,1,0:T(4,128)S(1)} %get-tuple-element.255), channel_id=1, source_target_pairs={{1,0},{2,1},{3,2},{4,3},{5,4},{6,5},{7,6},{8,7},{9,8},{10,9},{11,1... | collective-permute-start | bytes 147464 | tf_op jit(solution)/shard_map/ppermute | solution.py:29
  11.9 5.1 %copy-start.61 = (f32[38]{0:T(128)}, f32[38]{0:T(128)S(1)}, u32[]{:S(2)}) copy-start(f32[38]{0:T(128)S(1)} %and_convert_fusion.3) | copy-start | bytes 460
  11.9 6.9 %copy-start.52 = (f32[36]{0:T(128)}, f32[36]{0:T(128)S(1)}, u32[]{:S(2)}) copy-start(f32[36]{0:T(128)S(1)} %sine_multiply_fusion.2) | copy-start | bytes 436
  12.0 7.1 %copy-start.63 = (f32[36]{0:T(128)}, f32[36]{0:T(128)S(1)}, u32[]{:S(2)}) copy-start(f32[36]{0:T(128)S(1)} %and_convert_fusion.2) | copy-start | bytes 436
  12.0 8.8 %copy-start.54 = (f32[34]{0:T(128)}, f32[34]{0:T(128)S(1)}, u32[]{:S(2)}) copy-start(f32[34]{0:T(128)S(1)} %sine_multiply_fusion.1) | copy-start | bytes 412
  12.0 9.0 %copy-start.65 = (f32[34]{0:T(128)}, f32[34]{0:T(128)S(1)}, u32[]{:S(2)}) copy-start(f32[34]{0:T(128)S(1)} %and_convert_fusion.1) | copy-start | bytes 412
  12.6 2.5 %copy-start.10 = (f32[1,3,32,1024]{3,2,1,0:T(8,128)S(1)}, f32[1,3,32,1024]{3,2,1,0:T(8,128)}, u32[]{:S(2)}) copy-start(f32[1,3,32,1024]{3,2,1,0:T(8,128)} %param.4) | copy-start | bytes 1179652
  15.3 1.5 %copy-start.13 = (f32[3,38,1]{2,1,0:T(8,128)}, f32[3,38,1]{2,1,0:T(8,128)S(1)}, u32[]{:S(2)}) copy-start(f32[3,38,1]{2,1,0:T(8,128)S(1)} %get-tuple-element.228) | copy-start | bytes 1372
  17.2 1.6 %copy-start.15 = (f32[3,36,1]{2,1,0:T(8,128)}, f32[3,36,1]{2,1,0:T(8,128)S(1)}, u32[]{:S(2)}) copy-start(f32[3,36,1]{2,1,0:T(8,128)S(1)} %get-tuple-element.223) | copy-start | bytes 1300
  17.2 1.6 %copy-start.17 = (f32[3,36,1]{2,1,0:T(8,128)}, f32[3,36,1]{2,1,0:T(8,128)S(1)}, u32[]{:S(2)}) copy-start(f32[3,36,1]{2,1,0:T(8,128)S(1)} %get-tuple-element.224) | copy-start | bytes 1300
  17.5 1.3 copy-start
  19.2 1.6 %copy-start.19 = (f32[3,34,1]{2,1,0:T(8,128)}, f32[3,34,1]{2,1,0:T(8,128)S(1)}, u32[]{:S(2)}) copy-start(f32[3,34,1]{2,1,0:T(8,128)S(1)} %get-tuple-element.219) | copy-start | bytes 1228
  19.2 1.5 %copy-start.21 = (f32[3,34,1]{2,1,0:T(8,128)}, f32[3,34,1]{2,1,0:T(8,128)S(1)}, u32[]{:S(2)}) copy-start(f32[3,34,1]{2,1,0:T(8,128)S(1)} %get-tuple-element.220) | copy-start | bytes 1228
  19.5 1.3 copy-start.2
  19.5 1.3 copy-start.4
  21.2 1.9 %copy-start.32 = (f32[3,32,1]{2,1,0:T(8,128)}, f32[3,32,1]{2,1,0:T(8,128)S(1)}, u32[]{:S(2)}) copy-start(f32[3,32,1]{2,1,0:T(8,128)S(1)} %get-tuple-element.216) | copy-start | bytes 1156
  21.4 1.7 %copy-start.6 = (f32[3,32,1023]{2,1,0:T(8,128)}, f32[3,32,1023]{2,1,0:T(8,128)S(1)}, u32[]{:S(2)}) copy-start(f32[3,32,1023]{2,1,0:T(8,128)S(1)} %get-tuple-element.213) | copy-start | bytes 1178500
  21.4 1.7 %copy-start.8 = (f32[3,32,1023]{2,1,0:T(8,128)}, f32[3,32,1023]{2,1,0:T(8,128)S(1)}, u32[]{:S(2)}) copy-start(f32[3,32,1023]{2,1,0:T(8,128)S(1)} %get-tuple-element.214) | copy-start | bytes 1178500
  23.2 3.4 %copy-start.43 = (f32[1,4,32,1024]{3,2,1,0:T(8,128)S(1)}, f32[1,4,32,1024]{3,2,1,0:T(8,128)}, u32[]{:S(2)}) copy-start(f32[1,4,32,1024]{3,2,1,0:T(8,128)} %param.6) | copy-start | bytes 1572868
  23.4 1.3 copy-start.26
  23.4 3.3 %copy-start.12 = (f32[1,4,32,1024]{3,2,1,0:T(8,128)S(1)}, f32[1,4,32,1024]{3,2,1,0:T(8,128)}, u32[]{:S(2)}) copy-start(f32[1,4,32,1024]{3,2,1,0:T(8,128)} %convert_multiply_fusion) | copy-start | bytes 1572868
  24.7 33.0 %collective-permute-start.2 = (f32[3,32,1024]{2,1,0:T(8,128)}, f32[3,32,1024]{2,1,0:T(8,128)}, u32[]{:S(2)}, u32[]{:S(2)}) collective-permute-start(f32[3,32,1024]{2,1,0:T(8,128)} %maximum_multiply_fusion.3), channel_id=1, source_target_pairs={{0,16},{16,32},{32,48},{48,64},{64,80},{80,96},{96,112},{112,128},... | collective-permute-start | bytes 1179656 | tf_op jit(solution)/shard_map/ppermute | solution.py:39
  33.8 1.2 copy-start.24
  33.8 1.2 copy-start.27
  33.9 1.2 copy-start.30
  33.9 1.2 copy-start.59
  35.0 1.3 copy-start.7
  35.0 1.3 copy-start.33
  35.0 1.3 copy-start.57
  36.5 1.1 copy-start.49
  39.9 1.0 copy-start.22
  39.9 1.0 copy-start.55
  41.0 1.0 copy-start.3
  41.1 1.1 copy-start.40
  41.1 1.1 copy-start.46
  44.1 1.0 copy-start.53
  51.2 8.9 %collective-permute-start.4 = (f32[3,4,1024]{2,1,0:T(4,128)S(1)}, f32[3,4,1024]{2,1,0:T(4,128)S(1)}, u32[]{:S(2)}, u32[]{:S(2)}) collective-permute-start(f32[3,4,1024]{2,1,0:T(4,128)S(1)} %get-tuple-element.72), channel_id=1, source_target_pairs={{0,1},{1,2},{2,3},{3,4},{4,5},{5,6},{6,7},{7,8},{8,9},{9,10},{10,1... | collective-permute-start | bytes 147464 | tf_op jit(solution)/shard_map/ppermute | solution.py:27
  56.1 1.6 %copy-start.11 = (f32[1,3,32,1024]{3,2,1,0:T(8,128)S(1)}, f32[1,3,32,1024]{3,2,1,0:T(8,128)}, u32[]{:S(2)}) copy-start(f32[1,3,32,1024]{3,2,1,0:T(8,128)} %param.4) | copy-start | bytes 1179652
  56.1 1.6 %copy-start.50 = (f32[3,32,1024]{2,1,0:T(8,128)S(1)}, f32[3,32,1024]{2,1,0:T(8,128)}, u32[]{:S(2)}) copy-start(f32[3,32,1024]{2,1,0:T(8,128)} %param.5) | copy-start | bytes 1179652
  56.1 5.8 %collective-permute-start.5 = (f32[3,4,1024]{2,1,0:T(4,128)S(1)}, f32[3,4,1024]{2,1,0:T(4,128)S(1)}, u32[]{:S(2)}, u32[]{:S(2)}) collective-permute-start(f32[3,4,1024]{2,1,0:T(4,128)S(1)} %get-tuple-element.73), channel_id=1, source_target_pairs={{1,0},{2,1},{3,2},{4,3},{5,4},{6,5},{7,6},{8,7},{9,8},{10,9},{11,1... | collective-permute-start | bytes 147464 | tf_op jit(solution)/shard_map/ppermute | solution.py:29
  62.6 65.9 %copy-start.34 = (f32[3,32,1024]{2,1,0:T(8,128)}, f32[3,32,1024]{2,1,0:T(8,128)S(1)}, u32[]{:S(2)}) copy-start(f32[3,32,1024]{2,1,0:T(8,128)S(1)} %get-tuple-element.23) | copy-start | bytes 1179652
  128.4 15.7 %copy-start.25 = (f32[1,32,1024]{2,1,0:T(8,128)S(1)}, f32[1,32,1024]{2,1,0:T(8,128)}, u32[]{:S(2)}) copy-start(f32[1,32,1024]{2,1,0:T(8,128)} %copy-done.23) | copy-start | bytes 393220
  128.4 15.7 %copy-start.28 = (f32[1,32,1024]{2,1,0:T(8,128)S(1)}, f32[1,32,1024]{2,1,0:T(8,128)}, u32[]{:S(2)}) copy-start(f32[1,32,1024]{2,1,0:T(8,128)} %copy-done.26) | copy-start | bytes 393220
  128.4 15.7 %copy-start.31 = (f32[1,32,1024]{2,1,0:T(8,128)S(1)}, f32[1,32,1024]{2,1,0:T(8,128)}, u32[]{:S(2)}) copy-start(f32[1,32,1024]{2,1,0:T(8,128)} %copy-done.29) | copy-start | bytes 393220
  128.4 15.7 %copy-start.60 = (f32[32]{0:T(128)S(1)}, f32[32]{0:T(128)}, u32[]{:S(2)}) copy-start(f32[32]{0:T(128)} %and_convert_fusion) | copy-start | bytes 388
  128.5 15.6 %collective-permute-start.6 = (f32[3,32,1024]{2,1,0:T(8,128)S(1)}, f32[3,32,1024]{2,1,0:T(8,128)S(1)}, u32[]{:S(2)}, u32[]{:S(2)}) collective-permute-start(f32[3,32,1024]{2,1,0:T(8,128)S(1)} %divide_subtract_fusion), channel_id=1, source_target_pairs={{16,0},{32,16},{48,32},{64,48},{80,64},{96,80},{112,96},{128,112},... | collective-permute-start | bytes 1179656 | tf_op jit(solution)/shard_map/ppermute | solution.py:39
  (26 other events, 22.7 us)
where the time goes:
time: 146 us; the launch traced here: 145 us
  blocking collectives  65.1 us (45%)
  other arithmetic  23.9 us (16%)
  starting transfers between devices  20.6 us (14%)
  waiting for transfers between devices  15.2 us (10%)
  local copies, waits for them, and re-layouts  14.5 us (10%)
  between operations  5.63 us (4%)
    psum x5, blocking collectives, by_axis(): x = lax.psum(x, axis)  65.1 us
    ppermute x3, waiting for transfers between devices, from_behind(): return lax.ppermute(block, axis, route)  13.4 us
    ppermute x3, starting transfers between devices, from_behind(): return lax.ppermute(block, axis, route)  11.7 us
    unnamed x134, local copies, waits for them, and re-layouts  9.05 us
    ppermute x2, starting transfers between devices, extended_2(): lax.ppermute(tail, axis, [(i, (i + 1) % count) for i in range(ends)])  6.17 us
    add x4, other arithmetic, advance(): merid - half * (north[0] - south[0]) - coriolis * zonal  3.31 us
    mul x8, other arithmetic, section_rows(): return advance(current, coriolis_rows(index, total)) * valid  2.94 us
  transfers between devices with their start and end apart: 7, of which 2 were waited for; matrix products, arithmetic and copies ran while one was open for 19% of the time, Pallas kernels for 0%

commit v1 on v0

--- a/solution.py
+++ b/solution.py
@@ -41,7 +41,8 @@
 
 def by_axis(x, axes):
     for axis in axes:
-        x = lax.psum(x, axis)
+        pieces = lax.all_gather(x, axis, axis=0, tiled=False)
+        x = pieces.sum(axis=0)
     return x
 
 

time: 146 us -> 168 us (1.15)
  local copies, waits for them, and re-layouts: 14.5 us -> 34 us
  other arithmetic: 23.9 us -> 30.1 us
  waiting for transfers between devices: 15.2 us -> 12.5 us
  blocking collectives: 65.1 us -> 63.1 us
    psum x5 -> x0, blocking collectives: 65.1 us -> none  [by_axis(): x = lax.psum(x, axis)]
    unnamed x0 -> x5, blocking collectives: none -> 63.1 us
    unnamed x134 -> x159, local copies, waits for them, and re-layouts: 9.05 us -> 28.5 us
    reduce_sum x0 -> x10, other arithmetic: none -> 6.21 us  [by_axis(): x = pieces.sum(axis=0)]
    ppermute x2, waiting for transfers between devices: 1.82 us -> 0.01 us  [extended_2(): lax.ppermute(head, axis, [((i + 1) % count, i) for i in range(ends)])]
  transfers between devices with their start and end apart: 7 -> 7, of which waited for: 2 -> 1; matrix products, arithmetic and copies ran while one was open for 19% -> 19% of each run, Pallas kernels for 0% -> 0%
where the time goes in v1:
time: 168 us; the launch traced here: 166 us
  blocking collectives  63.1 us (38%)
  local copies, waits for them, and re-layouts  34 us (20%)
  other arithmetic  30.1 us (18%)
  starting transfers between devices  21 us (12%)
  waiting for transfers between devices  12.5 us (7%)
  between operations  5.72 us (3%)
    unnamed x5, blocking collectives  63.1 us
    unnamed x159, local copies, waits for them, and re-layouts  28.5 us
    ppermute x3, waiting for transfers between devices, from_behind(): return lax.ppermute(block, axis, route)  12.5 us
    ppermute x3, starting transfers between devices, from_behind(): return lax.ppermute(block, axis, route)  12 us
    ppermute x2, starting transfers between devices, extended_2(): lax.ppermute(tail, axis, [(i, (i + 1) % count) for i in range(ends)])  6.38 us
    reduce_sum x10, other arithmetic, by_axis(): x = pieces.sum(axis=0)  6.21 us
  transfers between devices with their start and end apart: 7, of which 1 were waited for; matrix products, arithmetic and copies ran while one was open for 19% of the time, Pallas kernels for 0%

profile of v1, /device:TPU:16, one launch (start us, length us, event | category | flops | bytes accessed | tf_op | source)
XLA Modules:
  0.0 166.4 jit_solution(9054715374704396468)
XLA Ops:
  0.6 7.6 %collective-permute-start.3 = (f32[3,32,1024]{2,1,0:T(8,128)}, f32[3,32,1024]{2,1,0:T(8,128)}, u32[]{:S(2)}, u32[]{:S(2)}) collective-permute-start(f32[3,32,1024]{2,1,0:T(8,128)} %bitcast.107), channel_id=1, source_target_pairs={{16,0},{32,16},{48,32},{64,48},{80,64},{96,80},{112,96},{128,112},... | collective-permute-start | bytes 1179656 | tf_op jit(solution)/shard_map/ppermute | solution.py:39
  8.2 1.0 fusion.121
  9.2 1.3 collective-permute-start.1
  10.5 3.0 %collective-permute-start = (f32[3,4,1024]{2,1,0:T(4,128)S(1)}, f32[3,4,1024]{2,1,0:T(4,128)S(1)}, u32[]{:S(2)}, u32[]{:S(2)}) collective-permute-start(f32[3,4,1024]{2,1,0:T(4,128)S(1)} %get-tuple-element.254), channel_id=1, source_target_pairs={{0,1},{1,2},{2,3},{3,4},{4,5},{5,6},{6,7},{7,8},{8,9},{9,10},{10,1... | collective-permute-start | bytes 147464 | tf_op jit(solution)/shard_map/ppermute | solution.py:27
  14.4 1.9 %convert_multiply_fusion = f32[1,4,32,1024]{3,2,1,0:T(8,128)} fusion(s32[1,4,32,1024]{3,2,1,0:T(8,128)} %param.7), kind=kLoop, calls=%fused_computation.32 | loop fusion | flops 262144 | bytes 1048576 | tf_op jit(solution)/shard_map/mul | solution.py:145
  16.8 1.3 dynamic-slice
  18.1 1.3 dynamic-slice.1
  20.2 0.8 fusion.41
  22.2 0.8 fusion.38
  24.2 0.8 fusion.35
  26.6 0.8 fusion.63
  28.1 0.8 maximum_multiply_fusion.3
  28.9 1.9 %collective-permute-start.2 = (f32[3,32,1024]{2,1,0:T(8,128)}, f32[3,32,1024]{2,1,0:T(8,128)}, u32[]{:S(2)}, u32[]{:S(2)}) collective-permute-start(f32[3,32,1024]{2,1,0:T(8,128)} %maximum_multiply_fusion.3), channel_id=1, source_target_pairs={{0,16},{16,32},{32,48},{48,64},{64,80},{80,96},{96,112},{112,128},... | collective-permute-start | bytes 1179656 | tf_op jit(solution)/shard_map/ppermute | solution.py:39
  30.9 2.4 %fusion.50 = (f32[]{:T(128)}, f32[]{:T(128)}, f32[]{:T(128)}, f32[]{:T(128)}, f32[32,1024]{1,0:T(8,128)}, /*index=5*/f32[32,1024]{1,0:T(8,128)S(1)}, f32[32,1024]{1,0:T(8,128)S(1)}) fusion(f32[3,32,1024]{2,1,0:T(8,128)} %maximum_multiply_fusion.3, f32[1,4,32,1024]{3,2,1,0:T(8,128)S(1)} %copy-done.12, f32[1,4,32,1024]{3,2,1,0:T(8,128)S(1)} %copy-done.43, ...), kind=kLoop, calls=%fused_computation.234 | loop fusion | flops 524284 | bytes 1966096 | tf_op jit(solution)/shard_map/reduce_sum | solution.py:119
  33.3 0.7 pad_bitcast_fusion
  37.2 0.9 pad_bitcast_fusion.2
  38.2 1.1 fusion.66
  39.4 1.2 add_multiply_fusion.3
  41.0 0.7 copy-done.9
  44.2 0.9 copy-done.5
  47.5 0.7 copy-done.48
  48.4 0.8 copy-done.1
  51.6 0.7 copy-done.47
  55.5 1.3 collective-permute-start.5
  56.8 3.3 %collective-permute-start.4 = (f32[3,4,1024]{2,1,0:T(4,128)S(1)}, f32[3,4,1024]{2,1,0:T(4,128)S(1)}, u32[]{:S(2)}, u32[]{:S(2)}) collective-permute-start(f32[3,4,1024]{2,1,0:T(4,128)S(1)} %get-tuple-element.72), channel_id=1, source_target_pairs={{0,1},{1,2},{2,3},{3,4},{4,5},{5,6},{6,7},{7,8},{8,9},{9,10},{10,1... | collective-permute-start | bytes 147464 | tf_op jit(solution)/shard_map/ppermute | solution.py:27
  60.3 1.7 %multiply_reduce_fusion = (f32[]{:T(128)}, f32[3,32,1024]{2,1,0:T(8,128)S(1)}) fusion(f32[3,32,1024]{2,1,0:T(8,128)S(1)} %copy-done.50, f32[3,32,1024]{2,1,0:T(8,128)} %collective-permute-done.2, pred[]{:T(512)S(6)} %eq.8, f32[1,3,32,1024]{3,2,1,0:T(8,128)S(1)} %copy-done.11), kind=kLoop, calls=%fused_computation.101 | loop fusion | flops 393215 | bytes 1572869 | tf_op jit(solution)/shard_map/reduce_sum | solution.py:153
  62.7 0.7 multiply_reduce_fusion.1
  63.4 1.4 dynamic-update-slice
  64.8 0.7 dynamic-update-slice.5
  65.6 35.2 %all-reduce.147 = (f32[16]{0:T(128)S(1)}, f32[16]{0:T(128)S(1)}) all-reduce(f32[16]{0:T(128)S(1)} %dynamic-update-slice, f32[16]{0:T(128)S(1)} %dynamic-update-slice.5), channel_id=1, replica_groups=mesh['tm_0'=16,'tm_1'=2,'lat_0'=4,'lat_1'=2,'lat_2'=2] {'tm_0'}, use_global_device_ids=true, to_apply=%add.137 | all-reduce | flops 32 | bytes 256
  102.0 1.3 dynamic-update-slice.1
  103.3 1.3 dynamic-update-slice.6
  104.6 1.3 dynamic-slice.2
  105.9 6.4 %all-reduce.151 = (f32[2]{0:T(128)S(1)}, f32[2]{0:T(128)S(1)}) all-reduce(f32[2]{0:T(128)S(1)} %dynamic-update-slice.1, f32[2]{0:T(128)S(1)} %dynamic-update-slice.6), channel_id=1, replica_groups=mesh['tm_0'=16,'tm_1'=2,'lat_0'=4,'lat_1'=2,'lat_2'=2] {'tm_1'}, use_global_device_ids=true, to_apply=%add.138 | all-reduce | flops 4 | bytes 32
  113.6 1.4 dynamic-update-slice.2
  115.0 1.4 dynamic-update-slice.7
  116.4 1.3 dynamic-slice.3
  117.6 14.1 %all-reduce.148 = (f32[4]{0:T(128)S(1)}, f32[4]{0:T(128)S(1)}) all-reduce(f32[4]{0:T(128)S(1)} %dynamic-update-slice.2, f32[4]{0:T(128)S(1)} %dynamic-update-slice.7), channel_id=1, replica_groups=mesh['tm_0'=16,'tm_1'=2,'lat_0'=4,'lat_1'=2,'lat_2'=2] {'lat_0'}, use_global_device_ids=true, to_apply=%add.139 | all-reduce | flops 8 | bytes 64
  133.0 1.4 dynamic-update-slice.3
  134.4 1.4 dynamic-update-slice.8
  135.8 1.3 dynamic-slice.4
  137.1 4.9 %all-reduce.150 = (f32[2]{0:T(128)S(1)}, f32[2]{0:T(128)S(1)}) all-reduce(f32[2]{0:T(128)S(1)} %dynamic-update-slice.3, f32[2]{0:T(128)S(1)} %dynamic-update-slice.8), channel_id=1, replica_groups=mesh['tm_0'=16,'tm_1'=2,'lat_0'=4,'lat_1'=2,'lat_2'=2] {'lat_1'}, use_global_device_ids=true, to_apply=%add.140 | all-reduce | flops 4 | bytes 32
  143.3 1.4 dynamic-update-slice.4
  144.7 1.4 dynamic-update-slice.9
  146.1 2.4 %all-reduce.149 = (f32[2]{0:T(128)S(1)}, f32[2]{0:T(128)S(1)}) all-reduce(f32[2]{0:T(128)S(1)} %dynamic-update-slice.4, f32[2]{0:T(128)S(1)} %dynamic-update-slice.9), channel_id=1, replica_groups=mesh['tm_0'=16,'tm_1'=2,'lat_0'=4,'lat_1'=2,'lat_2'=2] {'lat_2'}, use_global_device_ids=true, to_apply=%add.141 | all-reduce | flops 4 | bytes 32
  149.9 2.5 %collective-permute-start.6 = (f32[3,32,1024]{2,1,0:T(8,128)S(1)}, f32[3,32,1024]{2,1,0:T(8,128)S(1)}, u32[]{:S(2)}, u32[]{:S(2)}) collective-permute-start(f32[3,32,1024]{2,1,0:T(8,128)S(1)} %divide_subtract_fusion), channel_id=1, source_target_pairs={{16,0},{32,16},{48,32},{64,48},{80,64},{96,80},{112,96},{128,112},... | collective-permute-start | bytes 1179656 | tf_op jit(solution)/shard_map/ppermute | solution.py:39
  153.1 12.5 %collective-permute-done.6 = f32[3,32,1024]{2,1,0:T(8,128)S(1)} collective-permute-done((f32[3,32,1024]{2,1,0:T(8,128)S(1)}, f32[3,32,1024]{2,1,0:T(8,128)S(1)}, u32[]{:S(2)}, u32[]{:S(2)}) %collective-permute-start.6) | collective-permute-done | bytes 393248 | tf_op jit(solution)/shard_map/ppermute | solution.py:39
  165.5 0.9 select_bitcast_fusion
  (230 shorter events, 24.2 us)
Async XLA Ops:
  0.6 38.7 %collective-permute-start.3 = (f32[3,32,1024]{2,1,0:T(8,128)}, f32[3,32,1024]{2,1,0:T(8,128)}, u32[]{:S(2)}, u32[]{:S(2)}) collective-permute-start(f32[3,32,1024]{2,1,0:T(8,128)} %bitcast.107), channel_id=1, source_target_pairs={{16,0},{32,16},{48,32},{64,48},{80,64},{96,80},{112,96},{128,112},... | collective-permute-start | bytes 1179656 | tf_op jit(solution)/shard_map/ppermute | solution.py:39
  9.2 10.2 %collective-permute-start.1 = (f32[3,4,1024]{2,1,0:T(4,128)S(1)}, f32[3,4,1024]{2,1,0:T(4,128)S(1)}, u32[]{:S(2)}, u32[]{:S(2)}) collective-permute-start(f32[3,4,1024]{2,1,0:T(4,128)S(1)} %get-tuple-element.255), channel_id=1, source_target_pairs={{1,0},{2,1},{3,2},{4,3},{5,4},{6,5},{7,6},{8,7},{9,8},{10,9},{11,1... | collective-permute-start | bytes 147464 | tf_op jit(solution)/shard_map/ppermute | solution.py:29
  10.5 8.9 %collective-permute-start = (f32[3,4,1024]{2,1,0:T(4,128)S(1)}, f32[3,4,1024]{2,1,0:T(4,128)S(1)}, u32[]{:S(2)}, u32[]{:S(2)}) collective-permute-start(f32[3,4,1024]{2,1,0:T(4,128)S(1)} %get-tuple-element.254), channel_id=1, source_target_pairs={{0,1},{1,2},{2,3},{3,4},{4,5},{5,6},{6,7},{7,8},{8,9},{9,10},{10,1... | collective-permute-start | bytes 147464 | tf_op jit(solution)/shard_map/ppermute | solution.py:27
  13.6 7.7 %copy-start.61 = (f32[38]{0:T(128)}, f32[38]{0:T(128)S(1)}, u32[]{:S(2)}) copy-start(f32[38]{0:T(128)S(1)} %and_convert_fusion.3) | copy-start | bytes 460
  13.7 9.4 %copy-start.52 = (f32[36]{0:T(128)}, f32[36]{0:T(128)S(1)}, u32[]{:S(2)}) copy-start(f32[36]{0:T(128)S(1)} %sine_multiply_fusion.2) | copy-start | bytes 436
  13.7 9.6 %copy-start.63 = (f32[36]{0:T(128)}, f32[36]{0:T(128)S(1)}, u32[]{:S(2)}) copy-start(f32[36]{0:T(128)S(1)} %and_convert_fusion.2) | copy-start | bytes 436
  13.8 11.3 %copy-start.54 = (f32[34]{0:T(128)}, f32[34]{0:T(128)S(1)}, u32[]{:S(2)}) copy-start(f32[34]{0:T(128)S(1)} %sine_multiply_fusion.1) | copy-start | bytes 412
  13.8 11.5 %copy-start.65 = (f32[34]{0:T(128)}, f32[34]{0:T(128)S(1)}, u32[]{:S(2)}) copy-start(f32[34]{0:T(128)S(1)} %and_convert_fusion.1) | copy-start | bytes 412
  14.4 5.0 %copy-start.10 = (f32[1,3,32,1024]{3,2,1,0:T(8,128)S(1)}, f32[1,3,32,1024]{3,2,1,0:T(8,128)}, u32[]{:S(2)}) copy-start(f32[1,3,32,1024]{3,2,1,0:T(8,128)} %param.4) | copy-start | bytes 1179652
  19.6 1.5 copy-start.13
  21.5 1.6 copy-start.15
  21.5 1.5 copy-start.17
  21.7 1.3 copy-start
  23.5 1.6 copy-start.19
  23.5 1.5 copy-start.21
  23.7 1.3 copy-start.2
  23.7 1.3 copy-start.4
  25.5 1.9 %copy-start.32 = (f32[3,32,1]{2,1,0:T(8,128)}, f32[3,32,1]{2,1,0:T(8,128)S(1)}, u32[]{:S(2)}) copy-start(f32[3,32,1]{2,1,0:T(8,128)S(1)} %get-tuple-element.216) | copy-start | bytes 1156
  25.7 1.7 %copy-start.6 = (f32[3,32,1023]{2,1,0:T(8,128)}, f32[3,32,1023]{2,1,0:T(8,128)S(1)}, u32[]{:S(2)}) copy-start(f32[3,32,1023]{2,1,0:T(8,128)S(1)} %get-tuple-element.213) | copy-start | bytes 1178500
  25.7 1.7 %copy-start.8 = (f32[3,32,1023]{2,1,0:T(8,128)}, f32[3,32,1023]{2,1,0:T(8,128)S(1)}, u32[]{:S(2)}) copy-start(f32[3,32,1023]{2,1,0:T(8,128)S(1)} %get-tuple-element.214) | copy-start | bytes 1178500
  27.5 3.4 %copy-start.43 = (f32[1,4,32,1024]{3,2,1,0:T(8,128)S(1)}, f32[1,4,32,1024]{3,2,1,0:T(8,128)}, u32[]{:S(2)}) copy-start(f32[1,4,32,1024]{3,2,1,0:T(8,128)} %param.6) | copy-start | bytes 1572868
  27.6 1.3 copy-start.26
  27.6 3.2 %copy-start.12 = (f32[1,4,32,1024]{3,2,1,0:T(8,128)S(1)}, f32[1,4,32,1024]{3,2,1,0:T(8,128)}, u32[]{:S(2)}) copy-start(f32[1,4,32,1024]{3,2,1,0:T(8,128)} %convert_multiply_fusion) | copy-start | bytes 1572868
  28.9 31.4 %collective-permute-start.2 = (f32[3,32,1024]{2,1,0:T(8,128)}, f32[3,32,1024]{2,1,0:T(8,128)}, u32[]{:S(2)}, u32[]{:S(2)}) collective-permute-start(f32[3,32,1024]{2,1,0:T(8,128)} %maximum_multiply_fusion.3), channel_id=1, source_target_pairs={{0,16},{16,32},{32,48},{48,64},{64,80},{80,96},{96,112},{112,128},... | collective-permute-start | bytes 1179656 | tf_op jit(solution)/shard_map/ppermute | solution.py:39
  38.1 1.2 copy-start.24
  38.1 1.2 copy-start.27
  38.1 1.2 copy-start.30
  38.2 1.2 copy-start.59
  39.3 1.3 copy-start.7
  39.3 1.3 copy-start.33
  39.3 1.3 copy-start.57
  40.7 1.1 copy-start.49
  44.0 1.0 copy-start.55
  45.2 1.0 copy-start.3
  45.2 1.1 copy-start.40
  45.2 1.1 copy-start.46
  48.2 1.0 copy-start.18
  48.2 1.0 copy-start.53
  55.5 7.2 %collective-permute-start.5 = (f32[3,4,1024]{2,1,0:T(4,128)S(1)}, f32[3,4,1024]{2,1,0:T(4,128)S(1)}, u32[]{:S(2)}, u32[]{:S(2)}) collective-permute-start(f32[3,4,1024]{2,1,0:T(4,128)S(1)} %get-tuple-element.73), channel_id=1, source_target_pairs={{1,0},{2,1},{3,2},{4,3},{5,4},{6,5},{7,6},{8,7},{9,8},{10,9},{11,1... | collective-permute-start | bytes 147464 | tf_op jit(solution)/shard_map/ppermute | solution.py:29
  56.8 3.5 %copy-start.11 = (f32[1,3,32,1024]{3,2,1,0:T(8,128)S(1)}, f32[1,3,32,1024]{3,2,1,0:T(8,128)}, u32[]{:S(2)}) copy-start(f32[1,3,32,1024]{3,2,1,0:T(8,128)} %param.4) | copy-start | bytes 1179652
  56.8 3.5 %copy-start.50 = (f32[3,32,1024]{2,1,0:T(8,128)S(1)}, f32[3,32,1024]{2,1,0:T(8,128)}, u32[]{:S(2)}) copy-start(f32[3,32,1024]{2,1,0:T(8,128)} %param.5) | copy-start | bytes 1179652
  56.8 5.9 %collective-permute-start.4 = (f32[3,4,1024]{2,1,0:T(4,128)S(1)}, f32[3,4,1024]{2,1,0:T(4,128)S(1)}, u32[]{:S(2)}, u32[]{:S(2)}) collective-permute-start(f32[3,4,1024]{2,1,0:T(4,128)S(1)} %get-tuple-element.72), channel_id=1, source_target_pairs={{0,1},{1,2},{2,3},{3,4},{4,5},{5,6},{6,7},{7,8},{8,9},{9,10},{10,1... | collective-permute-start | bytes 147464 | tf_op jit(solution)/shard_map/ppermute | solution.py:27
  63.4 86.5 %copy-start.34 = (f32[3,32,1024]{2,1,0:T(8,128)}, f32[3,32,1024]{2,1,0:T(8,128)S(1)}, u32[]{:S(2)}) copy-start(f32[3,32,1024]{2,1,0:T(8,128)S(1)} %get-tuple-element.23) | copy-start | bytes 1179652
  149.8 15.7 %copy-start.25 = (f32[1,32,1024]{2,1,0:T(8,128)S(1)}, f32[1,32,1024]{2,1,0:T(8,128)}, u32[]{:S(2)}) copy-start(f32[1,32,1024]{2,1,0:T(8,128)} %copy-done.23) | copy-start | bytes 393220
  149.8 15.7 %copy-start.28 = (f32[1,32,1024]{2,1,0:T(8,128)S(1)}, f32[1,32,1024]{2,1,0:T(8,128)}, u32[]{:S(2)}) copy-start(f32[1,32,1024]{2,1,0:T(8,128)} %copy-done.26) | copy-start | bytes 393220
  149.8 15.7 %copy-start.31 = (f32[1,32,1024]{2,1,0:T(8,128)S(1)}, f32[1,32,1024]{2,1,0:T(8,128)}, u32[]{:S(2)}) copy-start(f32[1,32,1024]{2,1,0:T(8,128)} %copy-done.29) | copy-start | bytes 393220
  149.9 15.6 %collective-permute-start.6 = (f32[3,32,1024]{2,1,0:T(8,128)S(1)}, f32[3,32,1024]{2,1,0:T(8,128)S(1)}, u32[]{:S(2)}, u32[]{:S(2)}) collective-permute-start(f32[3,32,1024]{2,1,0:T(8,128)S(1)} %divide_subtract_fusion), channel_id=1, source_target_pairs={{16,0},{32,16},{48,32},{64,48},{80,64},{96,80},{112,96},{128,112},... | collective-permute-start | bytes 1179656 | tf_op jit(solution)/shard_map/ppermute | solution.py:39
  152.5 13.1 %copy-start.60 = (f32[32]{0:T(128)S(1)}, f32[32]{0:T(128)}, u32[]{:S(2)}) copy-start(f32[32]{0:T(128)} %and_convert_fusion) | copy-start | bytes 388
  (26 other events, 22.6 us)
